TPU v7x, 32 devices: a whole 2x2x4 slice. The times are simulated.
32 devices in a mesh: dp: 8 (over z, x), tensor: 4 (over y, core).
Axes of the slice: x: 2, y: 2, z: 4, core: 2. Of those that a mesh axis runs over, the one named last changes fastest.
Arguments:
- ranges: bfloat16 [10240, 2652], P('dp'), may hold values from 0.049804688 to 2
- pot: float32 [10240], P('dp'), may hold values from 0.1 to 1
- w_ranges: bfloat16 [2652, 2048], P(None, 'tensor'), may hold values from -0.125 to 0.125
- w_pot: float32 [2048], P('tensor'), may hold values from -5 to 5
- bias_one: float32 [2048], P('tensor'), may hold values from -1.5 to 1.5
- w_two: bfloat16 [2048, 2048], P('dp', 'tensor'), may hold values from -0.125 to 0.125
- bias_two: float32 [2048], P('tensor'), may hold values from -1.5 to 1.5
- w_three: bfloat16 [2048, 2048], P('dp', 'tensor'), may hold values from -0.125 to 0.125
- bias_three: float32 [2048], P('tensor'), may hold values from -1.5 to 1.5
- w_out: bfloat16 [2048, 2652], P(('dp', 'tensor')), may hold values from -0.1875 to 0.1875
- bias_out: float32 [2652], replicated, may hold values from -1.5 to 1.5
Outputs:
- hand_values: float32 [10240, 2652], P(('dp', 'tensor'))
All inputs are finite; a program needn't handle non-finite values.
Results may differ from a plain program's by a relative error of at most 0.0039.
Values may be sent and summed in bfloat16 or wider, within the bound.
A program may use at most 128 MiB of HBM per device.

v0:
```python
import jax
import jax.numpy as jnp
from jax import lax
from jax.sharding import PartitionSpec as P


def relu_round(pre):
    return jnp.maximum(pre, 0.0).astype(jnp.bfloat16)


def fold_rows(left, piece):
    return jnp.dot(left, piece, preferred_element_type=jnp.float32)


def local(
    ranges, pot, w_ranges, w_pot, bias_one, w_two, bias_two, w_three, bias_three, w_out, bias_out
):
    groups = lax.axis_size("tensor")
    position = lax.axis_index("tensor")
    states = ranges.shape[0]
    own_count = states // groups
    lowest = position * own_count
    own_ranges = lax.dynamic_slice_in_dim(ranges, lowest, own_count, 0)
    pre = jnp.dot(ranges, w_ranges, preferred_element_type=jnp.float32)
    hidden = relu_round(pre + pot[:, None] * w_pot[None, :] + bias_one[None, :])
    for weight, bias in ((w_two, bias_two), (w_three, bias_three)):
        whole = lax.all_gather(hidden, "tensor", axis=1, tiled=True)
        summed = fold_rows(whole, lax.all_gather(weight, "dp", axis=0, tiled=True))
        hidden = relu_round(summed + bias[None, :])
    own_hidden = lax.all_to_all(hidden, "tensor", split_axis=0, concat_axis=1, tiled=True)
    out_block = lax.all_gather(w_out, "tensor", axis=0, tiled=True)
    values = (
        fold_rows(own_hidden, lax.all_gather(out_block, "dp", axis=0, tiled=True))
        + bias_out[None, :]
    )
    weights = own_ranges.astype(jnp.float32)
    error = jnp.sum(weights * values, axis=1) / jnp.sum(weights, axis=1)
    return values - error[:, None]


def solution(mesh):
    in_specs = (
        P("dp", None),
        P("dp"),
        P(None, "tensor"),
        P("tensor"),
        P("tensor"),
        P("dp", "tensor"),
        P("tensor"),
        P("dp", "tensor"),
        P("tensor"),
        P(("dp", "tensor"), None),
        P(),
    )
    out_specs = P(("dp", "tensor"), None)
    return jax.shard_map(local, mesh=mesh, in_specs=in_specs, out_specs=out_specs, check_vma=False)
```

profile of v0, /device:TPU:1, one launch (start us, length us, event | category | flops | bytes accessed | tf_op | source)
XLA Modules:
  0.0 389.1 jit_solution(3218508177793755378)
XLA Ops:
  6.5 0.0 copy-start
  6.5 0.0 all-gather.9.cloned.1.call-start
  6.5 0.7 all-gather.9.cloned.1.call-update
  7.3 0.0 copy-start.2
  7.3 0.0 all-gather.7.cloned.1.call-start
  7.3 1.0 copy-done
  8.3 8.0 %fusion.5 = bf16[1280,512]{1,0:T(8,128)(2,1)} fusion(bf16[1280,2652]{0,1:T(8,128)(2,1)} %param.11, bf16[2652,512]{1,0:T(8,128)(2,1)S(1)} %copy-done, f32[512]{0:T(512)} %param.15, f32[512]{0:T(512)} %param.14, f32[1280]{0:T(1024)} %param.12), kind=kOutput, calls=%fused_computation.11 | convolution fusion | flops 3479306240 | bytes 10824704 | tf_op jit(solution)/shard_map/dot_general | solution.py:24
  16.3 0.0 all-gather.7.cloned.1.call-update
  16.4 0.0 all-gather.15.cloned.1.call-start
  16.4 0.7 all-gather.15.cloned.1.call-update
  17.1 0.0 all-gather.13.cloned.1.call-start
  17.2 0.5 all-gather.13.cloned.1.call-update
  17.7 0.0 all-gather.11.cloned.1.call-start
  17.7 41.0 %all-gather.9.cloned.1.call-done = bf16[2048,512]{1,0:T(8,128)(2,1)} async-done(((bf16[256,512]{1,0:T(8,128)(2,1)}), bf16[2048,512]{1,0:T(8,128)(2,1)}) %all-gather.9.cloned.1.call-update) | async-done | bytes 2097168 | tf_op jit(solution)/shard_map/all_gather | solution.py:28
  58.7 42.9 %all-gather.7.cloned.1.call-done = bf16[1280,2048]{1,0:T(8,128)(2,1)} async-done(((bf16[1280,512]{1,0:T(8,128)(2,1)}), bf16[1280,2048]{1,0:T(8,128)(2,1)}) %all-gather.7.cloned.1.call-update) | async-done | bytes 5242896 | tf_op jit(solution)/shard_map/all_gather | solution.py:27
  101.6 0.0 copy-done.2
  101.6 7.1 %fusion.6 = bf16[1280,512]{1,0:T(8,128)(2,1)} fusion(bf16[1280,2048]{1,0:T(8,128)(2,1)} %all-gather.7.cloned.1.call-done, bf16[2048,512]{1,0:T(8,128)(2,1)} %all-gather.9.cloned.1.call-done, f32[512]{0:T(512)S(1)} %copy-done.2), kind=kOutput, calls=%fused_computation.12 | convolution fusion | flops 2686320640 | bytes 8652800 | tf_op jit(solution)/shard_map/dot_general | solution.py:12
  108.7 0.0 copy-start.3
  108.7 0.0 all-gather.11.cloned.1.call-update
  108.7 0.0 all-gather.17.cloned.1.call-start
  108.8 12.9 %all-gather.15.cloned.1.call-done = bf16[256,2652]{1,0:T(8,128)(2,1)} async-done(((bf16[64,2652]{1,0:T(8,128)(2,1)}), bf16[256,2652]{1,0:T(8,128)(2,1)}) %all-gather.15.cloned.1.call-update) | async-done | bytes 1357840 | tf_op jit(solution)/shard_map/all_gather | solution.py:31
  121.7 0.0 all-gather.17.cloned.1.call-update
  121.7 48.8 %all-gather.13.cloned.1.call-done = bf16[2048,512]{1,0:T(8,128)(2,1)} async-done(((bf16[256,512]{1,0:T(8,128)(2,1)}), bf16[2048,512]{1,0:T(8,128)(2,1)}) %all-gather.13.cloned.1.call-update) | async-done | bytes 2097168 | tf_op jit(solution)/shard_map/all_gather | solution.py:28
  170.5 42.7 %all-gather.11.cloned.1.call-done = bf16[1280,2048]{1,0:T(8,128)(2,1)} async-done(((bf16[1280,512]{1,0:T(8,128)(2,1)}), bf16[1280,2048]{1,0:T(8,128)(2,1)}) %all-gather.11.cloned.1.call-update) | async-done | bytes 5242896 | tf_op jit(solution)/shard_map/all_gather | solution.py:27
  213.2 0.0 copy-done.3
  213.2 7.1 %fusion.7 = bf16[1280,512]{1,0:T(8,128)(2,1)} fusion(bf16[1280,2048]{1,0:T(8,128)(2,1)} %all-gather.11.cloned.1.call-done, bf16[2048,512]{1,0:T(8,128)(2,1)} %all-gather.13.cloned.1.call-done, f32[512]{0:T(512)S(1)} %copy-done.3), kind=kOutput, calls=%fused_computation.13 | convolution fusion | flops 2686320640 | bytes 8652800 | tf_op jit(solution)/shard_map/dot_general | solution.py:12
  220.3 4.6 %all-to-all-start = ((bf16[4,320,512]{2,1,0:T(8,128)(2,1)}), bf16[4,320,512]{2,1,0:T(8,128)(2,1)}, u32[]{:S(2)}, u32[]{:S(2)}) async-start(bf16[4,320,512]{2,1,0:T(8,128)(2,1)} %bitcast.12), calls=%async_computation | async-start | bytes 2621440 | tf_op jit(solution)/shard_map/all_to_all | solution.py:30
  224.9 4.6 %constant_dynamic-slice_fusion = bf16[320,2652]{0,1:T(8,128)(2,1)} fusion(bf16[1280,2652]{0,1:T(8,128)(2,1)} %param.11, s32[]{:T(128)S(6)} %select_n.3), kind=kLoop, calls=%fused_computation.15 | loop fusion | bytes 3394564 | tf_op jit(solution)/shard_map/dynamic_slice | solution.py:23
  229.5 0.0 copy-start.1
  229.5 4.0 %copy.17 = bf16[320,2652]{1,0:T(8,128)(2,1)} copy(bf16[320,2652]{0,1:T(8,128)(2,1)} %constant_dynamic-slice_fusion) | data formatting | bytes 3394560
  233.5 7.8 %all-to-all-done = bf16[4,320,512]{2,1,0:T(8,128)(2,1)} async-done(((bf16[4,320,512]{2,1,0:T(8,128)(2,1)}), bf16[4,320,512]{2,1,0:T(8,128)(2,1)}, u32[]{:S(2)}, u32[]{:S(2)}) %all-to-all-start) | async-done | bytes 1310752 | tf_op jit(solution)/shard_map/all_to_all | solution.py:30
  241.3 2.6 copy.18
  243.9 127.2 %all-gather.17.cloned.1.call-done = bf16[2048,2652]{1,0:T(8,128)(2,1)} async-done(((bf16[256,2652]{1,0:T(8,128)(2,1)}), bf16[2048,2652]{1,0:T(8,128)(2,1)}) %all-gather.17.cloned.1.call-update) | async-done | bytes 10862608 | tf_op jit(solution)/shard_map/all_gather | solution.py:33
  371.1 0.0 copy-done.1
  371.1 9.1 %convert_reduce_fusion = (f32[320]{0:T(512)S(1)}, f32[320]{0:T(512)S(1)}, f32[320,2652]{1,0:T(8,128)S(1)}) fusion(bf16[320,2652]{1,0:T(8,128)(2,1)} %copy.17, f32[2652]{0:T(1024)S(1)} %copy-done.1, bf16[320,2048]{1,0:T(8,128)(2,1)} %bitcast.13, bf16[2048,2652]{1,0:T(8,128)(2,1)} %all-gather.17.cloned.1.call-done), kind=kOutput, calls=%fused_computation | convolution fusion | flops 3480272128 | bytes 17278320 | tf_op jit(solution)/shard_map/dot_general | solution.py:12
  380.2 2.1 broadcast_subtract_fusion
  (1 shorter events, 0.0 us)
Async XLA Ops:
  6.5 1.8 copy-start
  6.5 52.2 %all-gather.9.cloned.1.call-start = ((), (), s32[]{:S(2)}) async-start(), calls=%async_computation.2 | async-start | bytes 2359296 | tf_op jit(solution)/shard_map/all_gather | solution.py:28
  7.3 94.3 %copy-start.2 = (f32[512]{0:T(512)S(1)}, f32[512]{0:T(512)}, u32[]{:S(2)}) copy-start(f32[512]{0:T(512)} %param.17) | copy-start | bytes 6148
  7.3 94.3 %all-gather.7.cloned.1.call-start = ((), (), s32[]{:S(2)}) async-start(), calls=%async_computation.1 | async-start | bytes 6553600 | tf_op jit(solution)/shard_map/all_gather | solution.py:27
  16.4 105.3 %all-gather.15.cloned.1.call-start = ((), (), s32[]{:S(2)}) async-start(), calls=%async_computation.5 | async-start | bytes 1720320 | tf_op jit(solution)/shard_map/all_gather | solution.py:31
  17.1 153.4 %all-gather.13.cloned.1.call-start = ((), (), s32[]{:S(2)}) async-start(), calls=%async_computation.4 | async-start | bytes 2359296 | tf_op jit(solution)/shard_map/all_gather | solution.py:28
  17.7 195.5 %all-gather.11.cloned.1.call-start = ((), (), s32[]{:S(2)}) async-start(), calls=%async_computation.3 | async-start | bytes 6553600 | tf_op jit(solution)/shard_map/all_gather | solution.py:27
  108.7 104.5 %copy-start.3 = (f32[512]{0:T(512)S(1)}, f32[512]{0:T(512)}, u32[]{:S(2)}) copy-start(f32[512]{0:T(512)} %param.19) | copy-start | bytes 6148
  108.7 262.3 %all-gather.17.cloned.1.call-start = ((), (), s32[]{:S(2)}) async-start(), calls=%async_computation.6 | async-start | bytes 12386304 | tf_op jit(solution)/shard_map/all_gather | solution.py:33
  220.3 21.0 %all-to-all-start = ((bf16[4,320,512]{2,1,0:T(8,128)(2,1)}), bf16[4,320,512]{2,1,0:T(8,128)(2,1)}, u32[]{:S(2)}, u32[]{:S(2)}) async-start(bf16[4,320,512]{2,1,0:T(8,128)(2,1)} %bitcast.12), calls=%async_computation | async-start | bytes 2621440 | tf_op jit(solution)/shard_map/all_to_all | solution.py:30
  229.5 141.6 %copy-start.1 = (f32[2652]{0:T(1024)S(1)}, f32[2652]{0:T(1024)}, u32[]{:S(2)}) copy-start(f32[2652]{0:T(1024)} %param.21) | copy-start | bytes 31828
Sparse Core Ops, SparseCore 0:
  9.5 49.2 all-gather.8
  60.3 41.2 all-gather.6
  103.2 18.5 all-gather.14
  123.7 46.7 all-gather.12
  171.9 41.2 all-gather.10
  215.2 155.7 all-gather.16
where the time goes:
time: 391 us; the launch traced here: 389 us
  waiting for transfers between devices  325 us (83%)
  matrix products  31.3 us (8%)
  between operations  13.5 us (3%)
  local copies, waits for them, and re-layouts  12.1 us (3%)
  starting transfers between devices  4.8 us (1%)
    all_gather x1, waiting for transfers between devices, local(): lax.all_gather(out_block, 'dp', axis=0, tiled=True)  127 us
    all_gather x2, waiting for transfers between devices, local(): summed = fold_rows(whole, lax.all_gather(weight, 'dp', axis=0, tiled=True))  89.8 us
    all_gather x2, waiting for transfers between devices, local(): whole = lax.all_gather(hidden, 'tensor', axis=1, tiled=True)  85.6 us
    dot_general x3, matrix products, fold_rows(): return jnp.dot(left, piece, preferred_element_type=jnp.float32)  23.3 us
    all_gather x1, waiting for transfers between devices, local(): out_block = lax.all_gather(w_out, 'tensor', axis=0, tiled=True)  12.9 us
    dot_general x1, matrix products, local(): pre = jnp.dot(ranges, w_ranges, preferred_element_type=jnp.float32)  8.04 us
    all_to_all x1, waiting for transfers between devices, local(): lax.all_to_all(hidden, 'tensor', split_axis=0, concat_axis=1, tiled=True)  7.82 us
  transfers between devices with their start and end apart: 7, of which 7 were waited for; matrix products, arithmetic and copies ran while one was open for 9% of the time, Pallas kernels for 0%

commit v1 on v0

v1 whole, which is shorter than its diff:
```python
import functools

import jax
import jax.numpy as jnp
from jax import lax
from jax.experimental import pallas as pl
from jax.experimental.pallas import tpu as pltpu
from jax.sharding import PartitionSpec as P

MESH = pl.DeviceIdType.MESH
CORES = 2


def relu_round(pre):
    return jnp.maximum(pre, 0.0).astype(jnp.bfloat16)


def fold_rows(left, piece):
    return jnp.dot(left, piece, preferred_element_type=jnp.float32)


def factors(dp, tensor):
    nx = max(f for f in range(1, dp + 1) if dp % f == 0 and f * f <= dp)
    return dp // nx, nx, tensor // CORES


def out_orders():
    return (("y", "z", "x"), ("y", "x", "z"))


def out_blocks(sizes):
    blocks = []
    for color, order in enumerate(out_orders()):
        for dy in range(sizes["y"]):
            for dz in range(sizes["z"]):
                for dx in range(sizes["x"]):
                    if color == 0:
                        when = 34 + 14 * dz + 8 * dx + dy
                    else:
                        when = 34 + 22 * dz + dy if dz else 17 + 12 * dx + dy
                    blocks.append((when, color, {"y": dy, "z": dz, "x": dx}))
    return sorted(blocks, key=lambda b: b[0])


def onward(order, sizes, far):
    axes = []
    for at, axis in enumerate(order):
        later = order[at + 1 :]
        if far[axis] < sizes[axis] - 1 and all(far[a] == 0 for a in later):
            axes.append(axis)
    return axes


def kernel(
    sizes, h_ref, w2_ref, w3_ref, wo_ref, b2_ref, b3_ref, third_ref, full_ref,
    act2, act3, stage2, stage3, w2_buf, w3_buf,
    w_send, w_recv, a_send, a_recv, p_recv, t_send, t_recv, o_send, o_recv, q_recv, own_sem,
):
    nz, nx, ny = sizes["z"], sizes["x"], sizes["y"]
    groups = ny * CORES
    dp_at, t_at = lax.axis_index("dp"), lax.axis_index("tensor")
    at = {
        "z": lax.div(dp_at, nx), "x": lax.rem(dp_at, nx),
        "y": lax.div(t_at, CORES), "c": lax.rem(t_at, CORES),
    }

    def shifted(axis, by):
        return lax.rem(at[axis] + by + sizes[axis], sizes[axis])

    def dev(z=None, x=None, y=None, c=None):
        z = at["z"] if z is None else z
        x = at["x"] if x is None else x
        y = at["y"] if y is None else y
        c = at["c"] if c is None else c
        return {"dp": z * nx + x, "tensor": y * CORES + c}

    nexts = {axis: dev(**{axis: shifted(axis, 1)}) for axis in ("z", "x", "y")}
    partner = dev(c=1 - at["c"])

    barrier = pltpu.get_barrier_semaphore()
    greeted = 0
    for axis in ("z", "x"):
        for by in {1 % sizes[axis], sizes[axis] - 1} - {0}:
            pl.semaphore_signal(
                barrier, inc=1, device_id=dev(**{axis: shifted(axis, by)}), device_id_type=MESH
            )
            greeted += 1
    for by in range(1, groups):
        pl.semaphore_signal(
            barrier, inc=1,
            device_id={"dp": dp_at, "tensor": lax.rem(t_at + by, groups)}, device_id_type=MESH,
        )
        greeted += 1
    pl.semaphore_wait(barrier, greeted)

    started = []

    def send(src, dst, s_sem, r_sem, to):
        copy = pltpu.make_async_remote_copy(
            src_ref=src, dst_ref=dst, send_sem=s_sem, recv_sem=r_sem,
            device_id=to, device_id_type=MESH,
        )
        copy.start()
        started.append(copy)

    def arrived(ref, sem, spare):
        pltpu.make_async_remote_copy(
            src_ref=ref, dst_ref=ref, send_sem=spare, recv_sem=sem,
            device_id=partner, device_id_type=MESH,
        ).wait_recv()

    def local_copy(src, dst, sem):
        copy = pltpu.make_async_copy(src, dst, sem)
        copy.start()
        return copy

    chunks, own, width = h_ref.shape
    depth = w2_ref.shape[0]
    sizes_w = {"z": nz, "x": nx}

    def columns(dy, core):
        piece = shifted("y", -dy) * CORES + core
        return pl.ds(pl.multiple_of(piece * width, width), width)

    def hidden_send(layer, j, dy, src):
        act = (act2, act3)[layer]
        spot = act.at[j, :, columns(dy, at["c"])]
        src = spot if src is None else src
        if dy < ny - 1:
            send(src, spot, a_send.at[layer, j, dy, 0], a_recv.at[layer, j, dy + 1], nexts["y"])
        send(src, spot, a_send.at[layer, j, dy, 1], p_recv.at[layer, j, dy], partner)

    def hidden_on(layer, j, dy):
        act = (act2, act3)[layer]
        arrived(act.at[j, :, columns(dy, at["c"])], a_recv.at[layer, j, dy], own_sem.at[0])
        hidden_send(layer, j, dy, None)

    def weight_rows(dz, dx):
        row = shifted("z", -dz) * nx + shifted("x", -dx)
        return pl.ds(pl.multiple_of(row * depth, depth), depth)

    def weight_on(layer, dz, dx):
        buf, ref = ((w2_buf, w2_ref), (w3_buf, w3_ref))[layer]
        spot = buf.at[weight_rows(dz, dx), :]
        src = spot
        if dz == 0 and dx == 0:
            src = ref
        else:
            arrived(spot, w_recv.at[layer, dz, dx], own_sem.at[0])
        for axis in onward(("z", "x"), sizes_w, {"z": dz, "x": dx}):
            to_z, to_x = (dz + 1, dx) if axis == "z" else (dz, dx + 1)
            which = 0 if axis == "z" else 1
            send(src, spot, w_send.at[layer, dz, dx, which], w_recv.at[layer, to_z, to_x], nexts[axis])

    def out_spot(color, far, core):
        row = shifted("z", -far["z"]) * nx + shifted("x", -far["x"])
        return full_ref.at[(row * groups + shifted("y", -far["y"]) * CORES + core) * 2 + color]

    def out_on(color, far, axes, wait, mate):
        order = out_orders()[color]
        spot = out_spot(color, far, at["c"])
        where = (color, far["y"], far["z"], far["x"])
        src = wo_ref.at[color] if sum(far.values()) == 0 else spot
        if wait and sum(far.values()):
            arrived(spot, o_recv.at[where], own_sem.at[0])
        for axis in onward(order, sizes, far):
            if axis not in axes:
                continue
            to = dict(far)
            to[axis] += 1
            send(
                src, spot, o_send.at[where + ("yzx".index(axis),)],
                o_recv.at[color, to["y"], to["z"], to["x"]], nexts[axis],
            )
        if mate:
            send(src, spot, o_send.at[where + (3,)], q_recv.at[where], partner)

    def compute(layer, j):
        act, buf, bias = ((act2, w2_buf, b2_ref), (act3, w3_buf, b3_ref))[layer]
        return relu_round(fold_rows(act[j], buf[...]) + bias[...])

    def pieces_here(layer, j):
        act = (act2, act3)[layer]
        for dy in range(ny):
            arrived(act.at[j, :, columns(dy, 1 - at["c"])], p_recv.at[layer, j, dy], own_sem.at[0])

    def layer_two(j):
        pieces_here(0, j)
        hidden = compute(0, j)
        stage2[j] = hidden
        act3[j, :, columns(0, at["c"])] = hidden
        hidden_send(1, j, 0, stage2.at[j])

    finals = []

    def layer_three(j):
        pieces_here(1, j)
        stage3[j] = compute(1, j)
        mine = third_ref.at[:, pl.ds(pl.multiple_of(t_at * width, width), width)]
        far = lax.rem(j - t_at + groups, groups)

        def away():
            return pltpu.make_async_remote_copy(
                src_ref=stage3.at[j], dst_ref=mine, send_sem=t_send.at[j], recv_sem=t_recv.at[far],
                device_id={"dp": dp_at, "tensor": jnp.int32(j)}, device_id_type=MESH,
            )

        def here():
            return pltpu.make_async_copy(stage3.at[j], mine, t_send.at[j])

        @pl.when(t_at != j)
        def _():
            away().start()

        @pl.when(t_at == j)
        def _():
            here().start()

        def finish():
            @pl.when(t_at != j)
            def _():
                away().wait_send()

            @pl.when(t_at == j)
            def _():
                here().wait()

        finals.append(finish)

    zero = {"y": 0, "z": 0, "x": 0}
    tasks = []
    for j in range(chunks):
        for dy in range(1, ny):
            tasks.append((9.0 * (j + 1) + 7 * (dy - 1), functools.partial(hidden_on, 0, j, dy)))
            tasks.append((36 + 7.0 * (j + 1) + 7 * (dy - 1), functools.partial(hidden_on, 1, j, dy)))
        last = 7 * (ny - 2)
        tasks.append((max(26, 9.0 * (j + 1) + last) + 0.1, functools.partial(layer_two, j)))
        tasks.append((36 + 7.0 * (j + 1) + last + 0.1, functools.partial(layer_three, j)))
    for layer, base in ((0, 0.0), (1, 17.0)):
        for dz in range(nz):
            for dx in range(nx):
                if dz + dx:
                    when = base + 5.6 * dz + (25 * layer + 25.9 if dx == nx - 1 else 6.0 * dx)
                    when = min(when, 25.95 if layer == 0 else 42.0)
                    tasks.append((when, functools.partial(weight_on, layer, dz, dx)))
    tasks.append((17.0, functools.partial(weight_on, 1, 0, 0)))
    for when, color, far in out_blocks(sizes):
        if sum(far.values()) == 0:
            tasks.append((16.5 if color else 33.0, functools.partial(out_on, color, far, "zx", False, False)))
        else:
            tasks.append((when, functools.partial(out_on, color, far, "yzx", True, True)))

    own_hidden = [
        local_copy(h_ref.at[j], act2.at[j, :, columns(0, at["c"])], own_sem.at[1 + j])
        for j in range(chunks)
    ]
    weight_on(0, 0, 0)
    for j in range(chunks):
        hidden_send(0, j, 0, h_ref.at[j])
        if j == 0:
            for color in range(2):
                out_on(color, zero, "y", False, True)
    own_out = [
        local_copy(wo_ref.at[color], out_spot(color, zero, at["c"]), own_sem.at[1 + chunks + color])
        for color in range(2)
    ]
    w2_buf[weight_rows(0, 0), :] = w2_ref[...]
    w3_buf[weight_rows(0, 0), :] = w3_ref[...]
    for copy in own_hidden:
        copy.wait()
    for _, task in sorted(tasks, key=lambda t: t[0]):
        task()

    for _, color, far in out_blocks(sizes):
        arrived(
            out_spot(color, far, 1 - at["c"]),
            q_recv.at[color, far["y"], far["z"], far["x"]], own_sem.at[0],
        )
    for by in range(1, groups):
        source = lax.rem(t_at - by + groups, groups)
        spot = third_ref.at[:, pl.ds(pl.multiple_of(source * width, width), width)]
        arrived(spot, t_recv.at[by], own_sem.at[0])
    for copy in own_out:
        copy.wait()
    for finish in finals:
        finish()
    for copy in started:
        copy.wait_send()


def middle(hidden, w_two, bias_two, w_three, bias_three, w_out):
    dp, groups = lax.axis_size("dp"), lax.axis_size("tensor")
    nz, nx, ny = factors(dp, groups)
    sizes = {"z": nz, "x": nx, "y": ny}
    states, width = hidden.shape
    own = states // groups
    rows, hands = w_out.shape
    units = width * groups
    vmem, anywhere = pl.BlockSpec(memory_space=pltpu.VMEM), pl.BlockSpec(memory_space=pl.ANY)
    dma = pltpu.SemaphoreType.DMA
    third, full = pl.pallas_call(
        functools.partial(kernel, sizes),
        out_shape=(
            jax.ShapeDtypeStruct((own, units), jnp.bfloat16),
            jax.ShapeDtypeStruct((dp * groups * 2, rows // 2, hands), jnp.bfloat16),
        ),
        in_specs=[anywhere, vmem, vmem, vmem, vmem, vmem],
        out_specs=(anywhere, anywhere),
        scratch_shapes=[
            pltpu.VMEM((groups, own, units), jnp.bfloat16),
            pltpu.VMEM((groups, own, units), jnp.bfloat16),
            pltpu.VMEM((groups, own, width), jnp.bfloat16),
            pltpu.VMEM((groups, own, width), jnp.bfloat16),
            pltpu.VMEM((units, width), jnp.bfloat16),
            pltpu.VMEM((units, width), jnp.bfloat16),
            dma((2, nz, nx, 2)),
            dma((2, nz, nx)),
            dma((2, groups, ny, 2)),
            dma((2, groups, ny)),
            dma((2, groups, ny)),
            dma((groups,)),
            dma((groups,)),
            dma((2, ny, nz, nx, 4)),
            dma((2, ny, nz, nx)),
            dma((2, ny, nz, nx)),
            dma((1 + groups + 2,)),
        ],
        compiler_params=pltpu.CompilerParams(
            collective_id=0, has_side_effects=True, vmem_limit_bytes=48 * 1024 * 1024
        ),
    )(
        hidden.reshape(groups, own, width), w_two, w_three, w_out.reshape(2, rows // 2, hands),
        bias_two[None, :], bias_three[None, :],
    )
    return third, full.reshape(units, hands)


def local(
    ranges, pot, w_ranges, w_pot, bias_one, w_two, bias_two, w_three, bias_three, w_out, bias_out
):
    groups = lax.axis_size("tensor")
    position = lax.axis_index("tensor")
    states = ranges.shape[0]
    own_count = states // groups
    lowest = position * own_count
    own_ranges = lax.dynamic_slice_in_dim(ranges, lowest, own_count, 0)
    pre = jnp.dot(ranges, w_ranges, preferred_element_type=jnp.float32)
    hidden = relu_round(pre + pot[:, None] * w_pot[None, :] + bias_one[None, :])
    own_hidden, out_whole = middle(hidden, w_two, bias_two, w_three, bias_three, w_out)
    values = fold_rows(own_hidden, out_whole) + bias_out[None, :]
    weights = own_ranges.astype(jnp.float32)
    error = jnp.sum(weights * values, axis=1) / jnp.sum(weights, axis=1)
    return values - error[:, None]


def solution(mesh):
    in_specs = (
        P("dp", None),
        P("dp"),
        P(None, "tensor"),
        P("tensor"),
        P("tensor"),
        P("dp", "tensor"),
        P("tensor"),
        P("dp", "tensor"),
        P("tensor"),
        P(("dp", "tensor"), None),
        P(),
    )
    out_specs = P(("dp", "tensor"), None)
    return jax.shard_map(local, mesh=mesh, in_specs=in_specs, out_specs=out_specs, check_vma=False)
```

time: 391 us -> 154 us (0.39)
  waiting for transfers between devices: 325 us -> 0 us
  Pallas kernels: 0 us -> 122 us
  matrix products: 31.3 us -> 16.8 us
  between operations: 13.5 us -> 0.06 us
  starting transfers between devices: 4.8 us -> 0 us
    all_gather x6 -> x0, waiting for transfers between devices: 315 us -> none  [the longest x1 127 us: local(): lax.all_gather(out_block, 'dp', axis=0, tiled=True)]
    pallas_call x0 -> x1, Pallas kernels: none -> 122 us  [middle(): pl.pallas_call(functools.partial(kernel, sizes), out_shape=(jax.ShapeDtyp...]
    dot_general x3 -> x1, matrix products: 23.3 us -> 8.74 us  [fold_rows(): return jnp.dot(left, piece, preferred_element_type=jnp.float32)]
    all_to_all x1 -> x0, waiting for transfers between devices: 7.82 us -> none  [local(): lax.all_to_all(hidden, 'tensor', split_axis=0, concat_axis=1, tiled=True)]
    all_to_all x1 -> x0, starting transfers between devices: 4.6 us -> none  [local(): lax.all_to_all(hidden, 'tensor', split_axis=0, concat_axis=1, tiled=True)]
    unnamed x9 -> x17, local copies, waits for them, and re-layouts: 5 us -> 8.12 us
  transfers between devices with their start and end apart: 7 -> 0, of which waited for: 7 -> 0; matrix products, arithmetic and copies ran while one was open for 9% -> 0% of each run, Pallas kernels for 0% -> 0%
where the time goes in v1:
time: 154 us
  Pallas kernels  122 us (79%)
  matrix products  16.8 us (11%)
  local copies, waits for them, and re-layouts  12.3 us (8%)
  other arithmetic  2.07 us (1%)
    pallas_call x1, Pallas kernels, middle(): pl.pallas_call(functools.partial(kernel, sizes), out_shape=(jax.ShapeDtyp...  122 us
    dot_general x1, matrix products, fold_rows(): return jnp.dot(left, piece, preferred_element_type=jnp.float32)  8.74 us
    unnamed x17, local copies, waits for them, and re-layouts  8.12 us
    dot_general x1, matrix products, local(): pre = jnp.dot(ranges, w_ranges, preferred_element_type=jnp.float32)  8.06 us
    dynamic_slice x1, local copies, waits for them, and re-layouts, local(): own_ranges = lax.dynamic_slice_in_dim(ranges, lowest, own_count, 0)  4.18 us

profile of v1, /device:TPU:1, one launch (start us, length us, event | category | flops | bytes accessed | tf_op | source)
XLA Modules:
  0.0 153.7 jit_solution(11466104123291217184)
XLA Ops:
  0.0 0.0 copy-start
  0.0 1.8 %copy-done = bf16[2652,512]{1,0:T(8,128)(2,1)S(1)} copy-done((bf16[2652,512]{1,0:T(8,128)(2,1)S(1)}, bf16[2652,512]{1,0:T(8,128)(2,1)}, u32[]{:S(2)}) %copy-start) | copy-done | bytes 2715672
  1.8 8.1 %fusion.3 = bf16[1280,512]{1,0:T(8,128)(2,1)} fusion(bf16[1280,2652]{0,1:T(8,128)(2,1)} %param.11, bf16[2652,512]{1,0:T(8,128)(2,1)S(1)} %copy-done, f32[512]{0:T(512)} %param.15, f32[512]{0:T(512)} %param.14, f32[1280]{0:T(1024)} %param.12), kind=kOutput, calls=%fused_computation.7 | convolution fusion | flops 3479306240 | bytes 10824704 | tf_op jit(solution)/shard_map/dot_general | solution.py:347
  9.8 4.2 %constant_dynamic-slice_fusion = bf16[320,2652]{0,1:T(8,128)(2,1)} fusion(bf16[1280,2652]{0,1:T(8,128)(2,1)} %param.11, s32[]{:T(128)S(6)} %select_n.3), kind=kLoop, calls=%fused_computation.9 | loop fusion | bytes 3394564 | tf_op jit(solution)/shard_map/dynamic_slice | solution.py:346
  14.0 0.0 copy-start.2
  14.0 0.0 copy-start.3
  14.0 0.0 copy-start.5
  14.0 0.0 copy-start.6
  14.0 0.0 copy-start.7
  14.0 4.1 %copy.13 = bf16[320,2652]{1,0:T(8,128)(2,1)} copy(bf16[320,2652]{0,1:T(8,128)(2,1)} %constant_dynamic-slice_fusion) | data formatting | bytes 3394560
  18.1 0.0 copy-done.2
  18.1 0.0 copy-done.3
  18.1 0.0 copy-done.5
  18.1 0.0 copy-done.6
  18.1 0.0 copy-start.1
  18.1 1.3 copy-done.1
  19.4 0.0 copy-start.4
  19.4 0.9 copy-done.4
  20.4 122.4 %shard_map.109 = (bf16[320,2048]{1,0:T(8,128)(2,1)S(1)}, bf16[64,32,2652]{2,1,0:T(8,128)(2,1)}) custom-call(bf16[4,320,512]{2,1,0:T(8,128)(2,1)S(1)} %bitcast.9, bf16[256,512]{1,0:T(8,128)(2,1)S(1)} %copy-done.3, bf16[256,512]{1,0:T(8,128)(2,1)S(1)} %copy-done.4, bf16[2,32,2652]{2,1,0:T(8,128)(2,1)S(1)} %bitcast.10, f32[1,512]{1,0:T(1,128)S(1)} %bitcast.11, ...), custom_call_target="tpu_custom_call" | custom-call | tf_op jit(solution)/shard_map/pallas_call | solution.py:301
  142.8 0.0 copy-done.7
  142.8 8.7 %convert_reduce_fusion = (f32[320]{0:T(512)S(1)}, f32[320]{0:T(512)S(1)}, f32[320,2652]{1,0:T(8,128)S(1)}) fusion(bf16[320,2652]{1,0:T(8,128)(2,1)} %copy.13, f32[2652]{0:T(1024)S(1)} %copy-done.7, bf16[320,2048]{1,0:T(8,128)(2,1)S(1)} %get-tuple-element.7, bf16[2048,2652]{1,0:T(8,128)(2,1)} %bitcast.13), kind=kOutput, calls=%fused_computation | convolution fusion | flops 3480272128 | bytes 17278320 | tf_op jit(solution)/shard_map/dot_general | solution.py:19
  151.6 2.1 %broadcast_subtract_fusion = f32[320,2652]{1,0:T(8,128)} fusion(f32[320,2652]{1,0:T(8,128)S(1)} %get-tuple-element.11, f32[320]{0:T(512)S(1)} %div.7), kind=kLoop, calls=%fused_computation.8 | loop fusion | flops 848640 | bytes 6790400 | tf_op jit(solution)/shard_map/sub | solution.py:353
  (1 shorter events, 0.0 us)
Async XLA Ops:
  0.0 1.8 %copy-start = (bf16[2652,512]{1,0:T(8,128)(2,1)S(1)}, bf16[2652,512]{1,0:T(8,128)(2,1)}, u32[]{:S(2)}) copy-start(bf16[2652,512]{1,0:T(8,128)(2,1)} %param.13) | copy-start | bytes 8146948
  14.0 4.1 %copy-start.2 = (bf16[64,2652]{1,0:T(8,128)(2,1)S(1)}, bf16[64,2652]{1,0:T(8,128)(2,1)}, u32[]{:S(2)}) copy-start(bf16[64,2652]{1,0:T(8,128)(2,1)} %param.20) | copy-start | bytes 1018372
  14.0 4.1 %copy-start.3 = (bf16[256,512]{1,0:T(8,128)(2,1)S(1)}, bf16[256,512]{1,0:T(8,128)(2,1)}, u32[]{:S(2)}) copy-start(bf16[256,512]{1,0:T(8,128)(2,1)} %w2_ref.1) | copy-start | bytes 786436
  14.0 4.1 %copy-start.5 = (f32[512]{0:T(512)S(1)}, f32[512]{0:T(512)}, u32[]{:S(2)}) copy-start(f32[512]{0:T(512)} %param.17) | copy-start | bytes 6148
  14.0 4.1 %copy-start.6 = (f32[512]{0:T(512)S(1)}, f32[512]{0:T(512)}, u32[]{:S(2)}) copy-start(f32[512]{0:T(512)} %param.19) | copy-start | bytes 6148
  14.0 128.8 %copy-start.7 = (f32[2652]{0:T(1024)S(1)}, f32[2652]{0:T(1024)}, u32[]{:S(2)}) copy-start(f32[2652]{0:T(1024)} %param.21) | copy-start | bytes 31828
  18.1 1.3 copy-start.1
  19.4 0.9 copy-start.4

commit v2 on v1

--- a/solution.py
+++ b/solution.py
@@ -1,4 +1,5 @@
 import functools
+import math
 
 import jax
 import jax.numpy as jnp
@@ -9,6 +10,8 @@
 
 MESH = pl.DeviceIdType.MESH
 CORES = 2
+STEP = 256
+W_ORDERS = (("z", "x"), ("x", "z"))
 
 
 def relu_round(pre):
@@ -25,7 +28,7 @@
 
 
 def out_orders():
-    return (("y", "z", "x"), ("y", "x", "z"))
+    return (("y", "z", "x"), ("y", "z", "x"))
 
 
 def out_blocks(sizes):
@@ -34,10 +37,7 @@
         for dy in range(sizes["y"]):
             for dz in range(sizes["z"]):
                 for dx in range(sizes["x"]):
-                    if color == 0:
-                        when = 34 + 14 * dz + 8 * dx + dy
-                    else:
-                        when = 34 + 22 * dz + dy if dz else 17 + 12 * dx + dy
+                    when = 20 + 18 * dz + 10 * color + 8 * dx + dy
                     blocks.append((when, color, {"y": dy, "z": dz, "x": dx}))
     return sorted(blocks, key=lambda b: b[0])
 
@@ -52,8 +52,9 @@
 
 
 def kernel(
-    sizes, h_ref, w2_ref, w3_ref, wo_ref, b2_ref, b3_ref, third_ref, full_ref,
-    act2, act3, stage2, stage3, w2_buf, w3_buf,
+    sizes, ranges_ref, wr_ref, pot_ref, wp_ref, b1_ref, w2_ref, w3_ref, wo_ref, b2_ref, b3_ref,
+    third_ref, full_ref, picked_ref,
+    ranges_buf, wr_buf, stage1, act2, act3, stage2, stage3, w2_buf, w3_buf,
     w_send, w_recv, a_send, a_recv, p_recv, t_send, t_recv, o_send, o_recv, q_recv, own_sem,
 ):
     nz, nx, ny = sizes["z"], sizes["x"], sizes["y"]
@@ -76,6 +77,21 @@
 
     nexts = {axis: dev(**{axis: shifted(axis, 1)}) for axis in ("z", "x", "y")}
     partner = dev(c=1 - at["c"])
+
+    states = ranges_ref.shape[1]
+    steps = states // math.gcd(states, STEP)
+    tall = states // steps
+    loads = [
+        pltpu.make_async_copy(
+            ranges_ref.at[:, pl.ds(i * tall, tall)], ranges_buf.at[:, pl.ds(i * tall, tall)],
+            own_sem.at[3 + i],
+        )
+        for i in range(steps)
+    ]
+    load_wr = pltpu.make_async_copy(wr_ref, wr_buf, own_sem.at[3 + steps])
+    load_wr.start()
+    for load in loads:
+        load.start()
 
     barrier = pltpu.get_barrier_semaphore()
     greeted = 0
@@ -114,7 +130,7 @@
         copy.start()
         return copy
 
-    chunks, own, width = h_ref.shape
+    chunks, own, width = stage2.shape
     depth = w2_ref.shape[0]
     sizes_w = {"z": nz, "x": nx}
 
@@ -147,7 +163,7 @@
             src = ref
         else:
             arrived(spot, w_recv.at[layer, dz, dx], own_sem.at[0])
-        for axis in onward(("z", "x"), sizes_w, {"z": dz, "x": dx}):
+        for axis in onward(W_ORDERS[layer], sizes_w, {"z": dz, "x": dx}):
             to_z, to_x = (dz + 1, dx) if axis == "z" else (dz, dx + 1)
             which = 0 if axis == "z" else 1
             send(src, spot, w_send.at[layer, dz, dx, which], w_recv.at[layer, to_z, to_x], nexts[axis])
@@ -191,6 +207,30 @@
         act3[j, :, columns(0, at["c"])] = hidden
         hidden_send(1, j, 0, stage2.at[j])
 
+    def layer_one(i):
+        if i == 0:
+            load_wr.wait()
+        loads[i].wait()
+        at_rows = pl.ds(i * tall, tall)
+        pre = lax.dot_general(
+            ranges_buf[:, at_rows], wr_buf[...], (((0,), (0,)), ((), ())),
+            preferred_element_type=jnp.float32,
+        )
+        stage1[at_rows, :] = relu_round(pre + pot_ref[at_rows, :] * wp_ref[...] + b1_ref[...])
+        for j in range(chunks):
+            if i * tall < (j + 1) * own <= (i + 1) * tall:
+                rows = pl.ds(j * own, own)
+                act2[j, :, columns(0, at["c"])] = stage1[rows, :]
+                hidden_send(0, j, 0, stage1.at[rows, :])
+
+    def pick():
+        wanted = lax.broadcasted_iota(jnp.int32, (own, states), 0) + t_at * own
+        found = lax.broadcasted_iota(jnp.int32, (own, states), 1) == wanted
+        picked_ref[...] = lax.dot_general(
+            jnp.where(found, 1.0, 0.0).astype(jnp.bfloat16), ranges_buf[...],
+            (((1,), (1,)), ((), ())), preferred_element_type=jnp.float32,
+        ).astype(jnp.bfloat16)
+
     finals = []
 
     def layer_three(j):
@@ -229,45 +269,38 @@
 
     zero = {"y": 0, "z": 0, "x": 0}
     tasks = []
+    last = 7 * (ny - 2)
+    for i in range(steps):
+        tasks.append((2.0 * i, functools.partial(layer_one, i)))
     for j in range(chunks):
         for dy in range(1, ny):
-            tasks.append((9.0 * (j + 1) + 7 * (dy - 1), functools.partial(hidden_on, 0, j, dy)))
-            tasks.append((36 + 7.0 * (j + 1) + 7 * (dy - 1), functools.partial(hidden_on, 1, j, dy)))
-        last = 7 * (ny - 2)
-        tasks.append((max(26, 9.0 * (j + 1) + last) + 0.1, functools.partial(layer_two, j)))
-        tasks.append((36 + 7.0 * (j + 1) + last + 0.1, functools.partial(layer_three, j)))
-    for layer, base in ((0, 0.0), (1, 17.0)):
-        for dz in range(nz):
-            for dx in range(nx):
-                if dz + dx:
-                    when = base + 5.6 * dz + (25 * layer + 25.9 if dx == nx - 1 else 6.0 * dx)
-                    when = min(when, 25.95 if layer == 0 else 42.0)
-                    tasks.append((when, functools.partial(weight_on, layer, dz, dx)))
-    tasks.append((17.0, functools.partial(weight_on, 1, 0, 0)))
+            tasks.append((4 + 9.0 * (j + 1) + 7 * (dy - 1), functools.partial(hidden_on, 0, j, dy)))
+            tasks.append((40 + 7.0 * (j + 1) + 7 * (dy - 1), functools.partial(hidden_on, 1, j, dy)))
+        tasks.append((max(30, 4 + 9.0 * (j + 1) + last) + 0.1, functools.partial(layer_two, j)))
+        tasks.append((40 + 7.0 * (j + 1) + last + 0.1, functools.partial(layer_three, j)))
+    tasks.append((41.0, pick))
+    for dz in range(nz):
+        for dx in range(nx):
+            if dz + dx:
+                when = 29.95 if dx == nx - 1 else 5.6 * dz + 6.0 * dx
+                tasks.append((when, functools.partial(weight_on, 0, dz, dx)))
+            when = 19 + 9.0 * dz + 0.1 * dx if dz else 5.5 + 6.0 * dx
+            tasks.append((when, functools.partial(weight_on, 1, dz, dx)))
     for when, color, far in out_blocks(sizes):
         if sum(far.values()) == 0:
-            tasks.append((16.5 if color else 33.0, functools.partial(out_on, color, far, "zx", False, False)))
+            tasks.append((17.0 + color, functools.partial(out_on, color, far, "zx", False, False)))
         else:
             tasks.append((when, functools.partial(out_on, color, far, "yzx", True, True)))
 
-    own_hidden = [
-        local_copy(h_ref.at[j], act2.at[j, :, columns(0, at["c"])], own_sem.at[1 + j])
-        for j in range(chunks)
-    ]
     weight_on(0, 0, 0)
-    for j in range(chunks):
-        hidden_send(0, j, 0, h_ref.at[j])
-        if j == 0:
-            for color in range(2):
-                out_on(color, zero, "y", False, True)
+    for color in range(2):
+        out_on(color, zero, "y", False, True)
     own_out = [
-        local_copy(wo_ref.at[color], out_spot(color, zero, at["c"]), own_sem.at[1 + chunks + color])
+        local_copy(wo_ref.at[color], out_spot(color, zero, at["c"]), own_sem.at[1 + color])
         for color in range(2)
     ]
     w2_buf[weight_rows(0, 0), :] = w2_ref[...]
     w3_buf[weight_rows(0, 0), :] = w3_ref[...]
-    for copy in own_hidden:
-        copy.wait()
     for _, task in sorted(tasks, key=lambda t: t[0]):
         task()
 
@@ -288,25 +321,32 @@
         copy.wait_send()
 
 
-def middle(hidden, w_two, bias_two, w_three, bias_three, w_out):
+def middle(
+    ranges, pot, w_ranges, w_pot, bias_one, w_two, bias_two, w_three, bias_three, w_out
+):
     dp, groups = lax.axis_size("dp"), lax.axis_size("tensor")
     nz, nx, ny = factors(dp, groups)
     sizes = {"z": nz, "x": nx, "y": ny}
-    states, width = hidden.shape
+    states, hands = ranges.shape
     own = states // groups
-    rows, hands = w_out.shape
+    width = w_ranges.shape[1]
+    rows = w_out.shape[0]
     units = width * groups
     vmem, anywhere = pl.BlockSpec(memory_space=pltpu.VMEM), pl.BlockSpec(memory_space=pl.ANY)
     dma = pltpu.SemaphoreType.DMA
-    third, full = pl.pallas_call(
+    third, full, picked = pl.pallas_call(
         functools.partial(kernel, sizes),
         out_shape=(
             jax.ShapeDtypeStruct((own, units), jnp.bfloat16),
             jax.ShapeDtypeStruct((dp * groups * 2, rows // 2, hands), jnp.bfloat16),
+            jax.ShapeDtypeStruct((own, hands), jnp.bfloat16),
         ),
-        in_specs=[anywhere, vmem, vmem, vmem, vmem, vmem],
-        out_specs=(anywhere, anywhere),
+        in_specs=[anywhere, anywhere] + [vmem] * 8,
+        out_specs=(anywhere, anywhere, vmem),
         scratch_shapes=[
+            pltpu.VMEM((hands, states), jnp.bfloat16),
+            pltpu.VMEM(w_ranges.shape, jnp.bfloat16),
+            pltpu.VMEM((states, width), jnp.bfloat16),
             pltpu.VMEM((groups, own, units), jnp.bfloat16),
             pltpu.VMEM((groups, own, units), jnp.bfloat16),
             pltpu.VMEM((groups, own, width), jnp.bfloat16),
@@ -323,30 +363,24 @@
             dma((2, ny, nz, nx, 4)),
             dma((2, ny, nz, nx)),
             dma((2, ny, nz, nx)),
-            dma((1 + groups + 2,)),
+            dma((4 + states // math.gcd(states, STEP),)),
         ],
         compiler_params=pltpu.CompilerParams(
-            collective_id=0, has_side_effects=True, vmem_limit_bytes=48 * 1024 * 1024
+            collective_id=0, has_side_effects=True, vmem_limit_bytes=56 * 1024 * 1024
         ),
     )(
-        hidden.reshape(groups, own, width), w_two, w_three, w_out.reshape(2, rows // 2, hands),
-        bias_two[None, :], bias_three[None, :],
+        ranges.T, w_ranges, pot[:, None], w_pot[None, :], bias_one[None, :],
+        w_two, w_three, w_out.reshape(2, rows // 2, hands), bias_two[None, :], bias_three[None, :],
     )
-    return third, full.reshape(units, hands)
+    return third, full.reshape(units, hands), picked
 
 
 def local(
     ranges, pot, w_ranges, w_pot, bias_one, w_two, bias_two, w_three, bias_three, w_out, bias_out
 ):
-    groups = lax.axis_size("tensor")
-    position = lax.axis_index("tensor")
-    states = ranges.shape[0]
-    own_count = states // groups
-    lowest = position * own_count
-    own_ranges = lax.dynamic_slice_in_dim(ranges, lowest, own_count, 0)
-    pre = jnp.dot(ranges, w_ranges, preferred_element_type=jnp.float32)
-    hidden = relu_round(pre + pot[:, None] * w_pot[None, :] + bias_one[None, :])
-    own_hidden, out_whole = middle(hidden, w_two, bias_two, w_three, bias_three, w_out)
+    own_hidden, out_whole, own_ranges = middle(
+        ranges, pot, w_ranges, w_pot, bias_one, w_two, bias_two, w_three, bias_three, w_out
+    )
     values = fold_rows(own_hidden, out_whole) + bias_out[None, :]
     weights = own_ranges.astype(jnp.float32)
     error = jnp.sum(weights * values, axis=1) / jnp.sum(weights, axis=1)

time: 154 us -> 140 us (0.909)
  local copies, waits for them, and re-layouts: 12.3 us -> 1.77 us
  matrix products: 16.8 us -> 9.31 us
  Pallas kernels: 122 us -> 127 us
    unnamed x17 -> x2, local copies, waits for them, and re-layouts: 8.12 us -> 0.01 us
    dot_general x1 -> x0, matrix products: 8.06 us -> none  [local(): pre = jnp.dot(ranges, w_ranges, preferred_element_type=jnp.float32)]
    pallas_call x1, Pallas kernels: 122 us -> 127 us  [middle(): pl.pallas_call(functools.partial(kernel, sizes), out_shape=(jax.ShapeDtyp...]
    dynamic_slice x1 -> x0, local copies, waits for them, and re-layouts: 4.18 us -> none  [local(): own_ranges = lax.dynamic_slice_in_dim(ranges, lowest, own_count, 0)]
    broadcast_in_dim x0 -> x1, local copies, waits for them, and re-layouts: none -> 1.77 us  [middle(): pot[:, None]]
where the time goes in v2:
time: 140 us
  Pallas kernels  127 us (91%)
  matrix products  9.31 us (7%)
  other arithmetic  2.07 us (1%)
  local copies, waits for them, and re-layouts  1.77 us (1%)
    pallas_call x1, Pallas kernels, middle(): pl.pallas_call(functools.partial(kernel, sizes), out_shape=(jax.ShapeDtyp...  127 us
    dot_general x1, matrix products, fold_rows(): return jnp.dot(left, piece, preferred_element_type=jnp.float32)  9.31 us

profile of v2, /device:TPU:1, one launch (start us, length us, event | category | flops | bytes accessed | tf_op | source)
XLA Modules:
  0.0 140.0 jit_solution(7269118393815530441)
XLA Ops:
  0.0 1.8 %broadcast_in_dim.22.pot_ref = f32[1280,1]{1,0:T(8,128)} reshape(f32[1280]{0:T(1024)} %param.12) | data formatting | bytes 10240 | tf_op jit(solution)/shard_map/broadcast_in_dim | solution.py:372
  1.8 0.0 copy-start
  1.8 126.8 %shard_map.109 = (bf16[320,2048]{1,0:T(8,128)(2,1)}, bf16[64,32,2652]{2,1,0:T(8,128)(2,1)}, bf16[320,2652]{1,0:T(8,128)(2,1)}) custom-call(bf16[2652,1280]{1,0:T(8,128)(2,1)} %bitcast.9, bf16[2652,512]{1,0:T(8,128)(2,1)} %wr_ref.1, f32[1280,1]{1,0:T(8,128)} %broadcast_in_dim.22.pot_ref, f32[1,512]{1,0:T(1,128)} %bitcast.11, f32[1,512]{1,0:T(1,128)} %bitcast.12, ...), custom_call_target="tpu_custom_call" | custom-call | tf_op jit(solution)/shard_map/pallas_call | solution.py:337
  128.6 0.0 copy-done
  128.6 9.3 %convert_reduce_fusion = (f32[320]{0:T(512)S(1)}, f32[320]{0:T(512)S(1)}, f32[320,2652]{1,0:T(8,128)S(1)}) fusion(bf16[320,2652]{1,0:T(8,128)(2,1)} %get-tuple-element.10, f32[2652]{0:T(1024)S(1)} %copy-done, bf16[320,2048]{1,0:T(8,128)(2,1)} %get-tuple-element.8, bf16[2048,2652]{1,0:T(8,128)(2,1)} %bitcast.15), kind=kOutput, calls=%fused_computation | convolution fusion | flops 3480272128 | bytes 17278320 | tf_op jit(solution)/shard_map/dot_general | solution.py:22
  137.9 2.1 %broadcast_subtract_fusion = f32[320,2652]{1,0:T(8,128)} fusion(f32[320,2652]{1,0:T(8,128)S(1)} %get-tuple-element.13, f32[320]{0:T(512)S(1)} %div.7), kind=kLoop, calls=%fused_computation.4 | loop fusion | flops 848640 | bytes 6790400 | tf_op jit(solution)/shard_map/sub | solution.py:387
  (1 shorter events, 0.0 us)
Async XLA Ops:
  1.8 126.8 %copy-start = (f32[2652]{0:T(1024)S(1)}, f32[2652]{0:T(1024)}, u32[]{:S(2)}) copy-start(f32[2652]{0:T(1024)} %param.21) | copy-start | bytes 31828

commit v3 on v2

--- a/solution.py
+++ b/solution.py
@@ -11,7 +11,7 @@
 MESH = pl.DeviceIdType.MESH
 CORES = 2
 STEP = 256
-W_ORDERS = (("z", "x"), ("x", "z"))
+W_ORDERS = (("z", "x"), ("z", "x"))
 
 
 def relu_round(pre):
@@ -28,18 +28,17 @@
 
 
 def out_orders():
-    return (("y", "z", "x"), ("y", "z", "x"))
+    return (("z", "y", "x"), ("x", "y", "z"))
 
 
 def out_blocks(sizes):
-    blocks = []
-    for color, order in enumerate(out_orders()):
-        for dy in range(sizes["y"]):
-            for dz in range(sizes["z"]):
-                for dx in range(sizes["x"]):
-                    when = 20 + 18 * dz + 10 * color + 8 * dx + dy
-                    blocks.append((when, color, {"y": dy, "z": dz, "x": dx}))
-    return sorted(blocks, key=lambda b: b[0])
+    return [
+        (color, {"y": dy, "z": dz, "x": dx})
+        for color in range(2)
+        for dy in range(sizes["y"])
+        for dz in range(sizes["z"])
+        for dx in range(sizes["x"])
+    ]
 
 
 def onward(order, sizes, far):
@@ -49,6 +48,108 @@
         if far[axis] < sizes[axis] - 1 and all(far[a] == 0 for a in later):
             axes.append(axis)
     return axes
+
+
+HOLDS = {("oy", 0): 27.9, ("oy", 1): 13.6, ("o", 0): 23.7, ("o", 1): 25.6, ("w", 1): 5.1, "load": 4.0}
+RANKS = {"hon": 0, "three": 1, "two": 1, "one": 2, "w": 3, "oy": 4, "o": 5, "pick": 9}
+
+
+def schedule(sizes, chunks, steps, firsts):
+    wire = {"x": 1.0, "y": 1.0, "z": 1.0, "c": 0.078}
+    delay = {"x": 1.8, "y": 1.8, "z": 2.6, "c": 1.0}
+    w_time, h_time, o_time = 5.6, 7.0, 3.64
+    nz, nx, ny = sizes["z"], sizes["x"], sizes["y"]
+    plan = {}
+    blocks = [(dz, dx) for dz in range(nz) for dx in range(nx)]
+
+    def further(far, axis):
+        return tuple(far[a] + (a == axis) for a in "yzx")
+
+    for layer in range(2):
+        for dz, dx in blocks:
+            far = {"z": dz, "x": dx, "y": 0}
+            sends = [
+                (a, w_time, ("w", layer) + further(far, a))
+                for a in onward(W_ORDERS[layer], sizes, far)
+            ]
+            first = (("hold", ("w", layer)),)
+            needs = (("w", layer, 0, dz, dx),) if dz + dx else first
+            plan["w", layer, dz, dx] = (needs, 0.05, sends)
+        for j in range(chunks):
+            for dy in range(1, ny):
+                sends = [("c", h_time, ("p", layer, j, dy))]
+                if dy < ny - 1:
+                    sends.append(("y", h_time, ("a", layer, j, dy + 1)))
+                plan["hon", layer, j, dy] = ((("a", layer, j, dy),), 0.05, sends)
+    for i in range(steps):
+        sends = []
+        for j in range(chunks):
+            if firsts[j] == i:
+                sends += [("y", h_time, ("a", 0, j, 1)), ("c", h_time, ("p", 0, j, 0))]
+        plan["one", i] = ((("hold", "load"),), 2.0, sends)
+    for j in range(chunks):
+        for layer, name in ((0, "two"), (1, "three")):
+            needs = [("p", layer, j, dy) for dy in range(ny)]
+            needs += [("done", ("w", layer) + block) for block in blocks]
+            needs += [("done", ("hon", layer, j, dy)) for dy in range(1, ny)]
+            needs.append(("done", ("two", j) if layer else ("one", firsts[j])))
+            sends = [("y", h_time / 2, ("t", j))]
+            if layer == 0:
+                sends = [("y", h_time, ("a", 1, j, 1)), ("c", h_time, ("p", 1, j, 0))]
+            plan[name, j] = (needs, 1.9, sends)
+    for color, far in out_blocks(sizes):
+        where = tuple(far[a] for a in "yzx")
+        sends = [
+            (a, o_time, ("o", color) + further(far, a))
+            for a in onward(out_orders()[color], sizes, far)
+        ]
+        mate = ("c", o_time, ("q", color) + where)
+        if sum(where):
+            plan[("o", color) + where] = ((("o", color) + where,), 0.05, sends + [mate])
+        else:
+            mine = [send for send in sends if send[0] == "y"] + [mate]
+            plan["oy", color] = ((("hold", ("oy", color)),), 0.05, mine)
+            rest = [send for send in sends if send[0] != "y"]
+            plan[("o", color) + where] = ((("hold", ("o", color)),), 0.05, rest)
+    plan["pick",] = (tuple(("done", ("one", i)) for i in range(steps)), 3.0, [])
+
+    free = dict.fromkeys(wire, 0.0)
+    there, done, order, now = {}, set(), [], 2.0
+
+    def ready(name):
+        at = now
+        for need in plan[name][0]:
+            if need[0] == "hold":
+                at = max(at, HOLDS.get(need[1], 0.0))
+            elif need[0] == "done":
+                if need[1] not in done:
+                    return None
+            elif need in there:
+                at = max(at, there[need])
+            else:
+                return None
+        return at
+
+    def rank(name):
+        tail = name[1:] if name[0] != "o" else (name[1], name[3], name[2], name[4])
+        return (RANKS[name[0]], name[1] if name[0] == "w" else 0) + tuple(tail)
+
+    todo = list(plan)
+    while todo:
+        open_now = [(ready(name), rank(name), name) for name in todo]
+        open_now = [entry for entry in open_now if entry[0] is not None]
+        soonest = min(entry[0] for entry in open_now)
+        at, _, name = min(
+            (entry for entry in open_now if entry[0] <= soonest + 1e-9), key=lambda entry: entry[1]
+        )
+        todo.remove(name)
+        now = at + plan[name][1]
+        done.add(name)
+        order.append(name)
+        for axis, cost, key in plan[name][2]:
+            free[axis] = max(free[axis], now) + cost * wire[axis]
+            there[key] = free[axis] + delay[axis]
+    return order
 
 
 def kernel(
@@ -131,6 +232,7 @@
         return copy
 
     chunks, own, width = stage2.shape
+    firsts = [((j + 1) * own - 1) // tall for j in range(chunks)]
     depth = w2_ref.shape[0]
     sizes_w = {"z": nz, "x": nx}
 
@@ -218,7 +320,7 @@
         )
         stage1[at_rows, :] = relu_round(pre + pot_ref[at_rows, :] * wp_ref[...] + b1_ref[...])
         for j in range(chunks):
-            if i * tall < (j + 1) * own <= (i + 1) * tall:
+            if firsts[j] == i:
                 rows = pl.ds(j * own, own)
                 act2[j, :, columns(0, at["c"])] = stage1[rows, :]
                 hidden_send(0, j, 0, stage1.at[rows, :])
@@ -268,43 +370,34 @@
         finals.append(finish)
 
     zero = {"y": 0, "z": 0, "x": 0}
-    tasks = []
-    last = 7 * (ny - 2)
-    for i in range(steps):
-        tasks.append((2.0 * i, functools.partial(layer_one, i)))
-    for j in range(chunks):
-        for dy in range(1, ny):
-            tasks.append((4 + 9.0 * (j + 1) + 7 * (dy - 1), functools.partial(hidden_on, 0, j, dy)))
-            tasks.append((40 + 7.0 * (j + 1) + 7 * (dy - 1), functools.partial(hidden_on, 1, j, dy)))
-        tasks.append((max(30, 4 + 9.0 * (j + 1) + last) + 0.1, functools.partial(layer_two, j)))
-        tasks.append((40 + 7.0 * (j + 1) + last + 0.1, functools.partial(layer_three, j)))
-    tasks.append((41.0, pick))
-    for dz in range(nz):
-        for dx in range(nx):
-            if dz + dx:
-                when = 29.95 if dx == nx - 1 else 5.6 * dz + 6.0 * dx
-                tasks.append((when, functools.partial(weight_on, 0, dz, dx)))
-            when = 19 + 9.0 * dz + 0.1 * dx if dz else 5.5 + 6.0 * dx
-            tasks.append((when, functools.partial(weight_on, 1, dz, dx)))
-    for when, color, far in out_blocks(sizes):
-        if sum(far.values()) == 0:
-            tasks.append((17.0 + color, functools.partial(out_on, color, far, "zx", False, False)))
-        else:
-            tasks.append((when, functools.partial(out_on, color, far, "yzx", True, True)))
-
-    weight_on(0, 0, 0)
-    for color in range(2):
-        out_on(color, zero, "y", False, True)
     own_out = [
         local_copy(wo_ref.at[color], out_spot(color, zero, at["c"]), own_sem.at[1 + color])
         for color in range(2)
     ]
     w2_buf[weight_rows(0, 0), :] = w2_ref[...]
     w3_buf[weight_rows(0, 0), :] = w3_ref[...]
-    for _, task in sorted(tasks, key=lambda t: t[0]):
-        task()
-
-    for _, color, far in out_blocks(sizes):
+    for name in schedule(sizes, chunks, steps, firsts):
+        kind = name[0]
+        if kind == "w":
+            weight_on(*name[1:])
+        elif kind == "hon":
+            hidden_on(*name[1:])
+        elif kind == "one":
+            layer_one(name[1])
+        elif kind == "two":
+            layer_two(name[1])
+        elif kind == "three":
+            layer_three(name[1])
+        elif kind == "pick":
+            pick()
+        elif kind == "oy":
+            out_on(name[1], zero, "y", False, True)
+        else:
+            far = dict(zip("yzx", name[2:]))
+            mine = sum(name[2:]) == 0
+            out_on(name[1], far, "zx" if mine else "yzx", not mine, not mine)
+
+    for color, far in out_blocks(sizes):
         arrived(
             out_spot(color, far, 1 - at["c"]),
             q_recv.at[color, far["y"], far["z"], far["x"]], own_sem.at[0],

time: 140 us -> 120 us (0.86)
  Pallas kernels: 127 us -> 106 us
    pallas_call x1, Pallas kernels: 127 us -> 106 us  [middle(): pl.pallas_call(functools.partial(kernel, sizes), out_shape=(jax.ShapeDtyp...]
where the time goes in v3:
time: 120 us
  Pallas kernels  106 us (88%)
  matrix products  9.29 us (8%)
  other arithmetic  2.07 us (2%)
  local copies, waits for them, and re-layouts  1.77 us (1%)
    pallas_call x1, Pallas kernels, middle(): pl.pallas_call(functools.partial(kernel, sizes), out_shape=(jax.ShapeDtyp...  106 us
    dot_general x1, matrix products, fold_rows(): return jnp.dot(left, piece, preferred_element_type=jnp.float32)  9.29 us

profile of v3, /device:TPU:1, one launch (start us, length us, event | category | flops | bytes accessed | tf_op | source)
XLA Modules:
  0.0 119.5 jit_solution(13824365721565375871)
XLA Ops:
  0.0 1.8 %broadcast_in_dim.22.pot_ref = f32[1280,1]{1,0:T(8,128)} reshape(f32[1280]{0:T(1024)} %param.12) | data formatting | bytes 10240 | tf_op jit(solution)/shard_map/broadcast_in_dim | solution.py:465
  1.8 0.0 copy-start
  1.8 106.4 %shard_map.109 = (bf16[320,2048]{1,0:T(8,128)(2,1)}, bf16[64,32,2652]{2,1,0:T(8,128)(2,1)}, bf16[320,2652]{1,0:T(8,128)(2,1)}) custom-call(bf16[2652,1280]{1,0:T(8,128)(2,1)} %bitcast.9, bf16[2652,512]{1,0:T(8,128)(2,1)} %wr_ref.1, f32[1280,1]{1,0:T(8,128)} %broadcast_in_dim.22.pot_ref, f32[1,512]{1,0:T(1,128)} %bitcast.11, f32[1,512]{1,0:T(1,128)} %bitcast.12, ...), custom_call_target="tpu_custom_call" | custom-call | tf_op jit(solution)/shard_map/pallas_call | solution.py:430
  108.2 0.0 copy-done
  108.2 9.3 %convert_reduce_fusion = (f32[320]{0:T(512)S(1)}, f32[320]{0:T(512)S(1)}, f32[320,2652]{1,0:T(8,128)S(1)}) fusion(bf16[320,2652]{1,0:T(8,128)(2,1)} %get-tuple-element.10, f32[2652]{0:T(1024)S(1)} %copy-done, bf16[320,2048]{1,0:T(8,128)(2,1)} %get-tuple-element.8, bf16[2048,2652]{1,0:T(8,128)(2,1)} %bitcast.15), kind=kOutput, calls=%fused_computation | convolution fusion | flops 3480272128 | bytes 17278320 | tf_op jit(solution)/shard_map/dot_general | solution.py:22
  117.5 2.1 %broadcast_subtract_fusion = f32[320,2652]{1,0:T(8,128)} fusion(f32[320,2652]{1,0:T(8,128)S(1)} %get-tuple-element.13, f32[320]{0:T(512)S(1)} %div.7), kind=kLoop, calls=%fused_computation.4 | loop fusion | flops 848640 | bytes 6790400 | tf_op jit(solution)/shard_map/sub | solution.py:480
  (1 shorter events, 0.0 us)
Async XLA Ops:
  1.8 106.4 %copy-start = (f32[2652]{0:T(1024)S(1)}, f32[2652]{0:T(1024)}, u32[]{:S(2)}) copy-start(f32[2652]{0:T(1024)} %param.21) | copy-start | bytes 31828
